TPU v7x, 32 devices: a whole 2x2x4 slice. The times are simulated.
32 devices in a mesh: batch: 8 (over z, x), head: 4 (over y, core).
Axes of the slice: x: 2, y: 2, z: 4, core: 2. Of those that a mesh axis runs over, the one named last changes fastest.
Arguments:
- features: bfloat16 [1024, 24, 512], P(('batch', 'head')), may hold values from -6 to 6
- state_h: bfloat16 [1024, 1024], P(('batch', 'head')), may hold values from -0.8984375 to 0.8984375
- state_c: bfloat16 [1024, 1024], P(('batch', 'head')), may hold values from -4 to 4
- valid: int32 [1024], P(('batch', 'head')), may hold values 0 or 1
- ends: int32 [1024, 24], P(('batch', 'head')), may hold values 0 or 1
- policy: int32 [1024, 1], P(('batch', 'head')), may hold values from 0 to 31; in each aligned block of 32 rows (0 to 31, 32 to 63, ...) at most 2 rows name the same one
- actions: int32 [1024, 16], P(('batch', 'head')), may hold values from 0 to 17
- w_input: bfloat16 [512, 4, 1024], P('batch', None, 'head'), may hold values from -0.25 to 0.25
- w_recur: bfloat16 [1024, 4, 1024], P('batch', None, 'head'), may hold values from -0.1875 to 0.1875
- lstm_bias: float32 [4, 1024], replicated, may hold values from -3 to 5
- w_hidden: bfloat16 [32, 1024, 1024], P('head'), may hold values from -0.1875 to 0.1875
- w_value: bfloat16 [32, 512], P('head'), may hold values from -0.25 to 0.25
- w_advantage: bfloat16 [32, 512, 18], P('head'), may hold values from -0.25 to 0.25
Outputs:
- q_values: float32 [1024, 16, 18], P(('batch', 'head'))
- q_taken: float32 [1024, 16], P(('batch', 'head'))
Inputs may be any that keep to these rules, and one draw needn't show every extreme that they name: In the rows of one device no policy appears more than 2 times, and some policy appears exactly 2 times.
All inputs are finite; a program needn't handle non-finite values. No bound on the sum of `valid` or of `ends` on one device may be relied on, other than what follows from the above.
Results may differ from a plain program's by a relative error of at most 0.007.
Values may be sent and summed in bfloat16 or wider, within the bound.
No kernel may reach another device: no remote copies, remote signals or barrier semaphores. Data moves between devices by JAX's collectives and lax.ppermute only.
A program may use at most 128 MiB of HBM per device.

v0:
```python
import jax
import jax.numpy as jnp
from jax import lax
from jax.sharding import PartitionSpec as P

ACTIONS = 18
POLICIES = 32
CAPP = 2


def slot_table(owners, per_source, capacity, policies):
    count = owners.shape[0]
    sources = count // per_source
    place = jnp.arange(count, dtype=jnp.int32)
    anchor = place // per_source
    before = (
        (owners[:, None] == owners[None, :])
        & (anchor[:, None] == anchor[None, :])
        & (place[None, :] < place[:, None])
    )
    rank = jnp.sum(before.astype(jnp.int32), axis=1)
    target = owners * (sources * capacity) + anchor * capacity + rank
    total = policies * sources * capacity
    return (jnp.arange(total, dtype=jnp.int32)[:, None] == target[None, :]).astype(jnp.bfloat16)


def lstm_cell(pre_t, full_h, cell_state, keep_t, w_flat, bias, width):
    full_h = full_h * keep_t[:, None].astype(jnp.bfloat16)
    cell_state = cell_state * keep_t[:, None]
    gates = (
        pre_t
        + jnp.dot(full_h, w_flat, preferred_element_type=jnp.float32).reshape(-1, 4, width)
        + bias
    )
    cell_state = jax.nn.sigmoid(gates[:, 1]) * cell_state + jax.nn.sigmoid(gates[:, 0]) * jnp.tanh(
        gates[:, 2]
    )
    new_h = (jax.nn.sigmoid(gates[:, 3]) * jnp.tanh(cell_state)).astype(jnp.bfloat16)
    return (new_h, cell_state)


def shards(
    features,
    state_h,
    state_c,
    valid,
    ends,
    policy,
    actions,
    w_input,
    w_recur,
    lstm_bias,
    w_hidden,
    w_value,
    w_advantage,
):
    seq_dev, steps, width_e = features.shape
    width_h = state_h.shape[1]
    learn = actions.shape[1]
    burn = steps - learn
    heads_n = lax.axis_size("head")
    keep_start = valid.astype(jnp.bfloat16)[:, None]
    start_h = state_h * keep_start
    start_c = state_c * keep_start
    quarter = width_h // heads_n
    place = lax.axis_index("head")
    w_in_part, w_rec_part = (
        lax.all_gather(w_input, "batch", axis=0, tiled=True),
        lax.all_gather(w_recur, "batch", axis=0, tiled=True),
    )
    feats, ends_group, owners_group, group_h, group_c = (
        lax.all_gather(features, "head", axis=0, tiled=True),
        lax.all_gather(ends.astype(jnp.bfloat16), "head", axis=0, tiled=True),
        lax.all_gather(policy.astype(jnp.bfloat16), "head", axis=0, tiled=True),
        lax.all_gather(start_h, "head", axis=0, tiled=True),
        lax.all_gather(start_c, "head", axis=0, tiled=True),
    )
    group = feats.shape[0]
    pre = jnp.dot(
        feats.transpose(1, 0, 2).reshape(-1, width_e),
        w_in_part.reshape(width_e, 4 * quarter),
        preferred_element_type=jnp.float32,
    ).reshape(steps, group, 4, quarter)
    bias = lax.dynamic_slice_in_dim(lstm_bias, place * quarter, quarter, 1)
    part_h = lax.dynamic_slice_in_dim(group_h, place * quarter, quarter, 1)
    part_c = lax.dynamic_slice_in_dim(group_c, place * quarter, quarter, 1).astype(jnp.float32)
    w_flat = w_rec_part.reshape(width_h, 4 * quarter)
    keeps = 1.0 - ends_group.astype(jnp.float32).T

    def advance(carry, inputs):
        part_h, part_c = carry
        pre_t, keep_t = inputs
        full_h = lax.all_gather(part_h, "head", axis=1, tiled=True)
        new_h, part_c = lstm_cell(pre_t, full_h, part_c, keep_t, w_flat, bias, quarter)
        return ((new_h, part_c), new_h)

    _, outputs = lax.scan(advance, (part_h, part_c), (pre, keeps))
    learned = outputs[burn:]
    table = slot_table(owners_group[:, 0].astype(jnp.int32), seq_dev, CAPP, POLICIES)
    packed = jnp.einsum("ks,tsu->ktu", table, learned, preferred_element_type=jnp.float32).astype(
        jnp.bfloat16
    )
    packed = packed.reshape(POLICIES, heads_n * CAPP, learn, quarter)
    routed = lax.all_to_all(packed, "head", split_axis=0, concat_axis=3, tiled=True)
    local_heads, slots = (routed.shape[0], routed.shape[1])
    rows = routed.reshape(local_heads, slots * learn, width_h)
    mid = jnp.einsum("prh,phk->prk", rows, w_hidden, preferred_element_type=jnp.float32)
    mid = jnp.maximum(mid, 0.0).astype(jnp.bfloat16)
    branch = w_value.shape[1]
    value = jnp.einsum(
        "prk,pk->pr", mid[:, :, :branch], w_value, preferred_element_type=jnp.float32
    )
    advantage = jnp.einsum(
        "prk,pka->pra", mid[:, :, branch:], w_advantage, preferred_element_type=jnp.float32
    )
    q_local = value[:, :, None] + advantage - jnp.mean(advantage, axis=-1, keepdims=True)
    q_local = q_local.reshape(local_heads, slots, learn, ACTIONS)
    returned = lax.all_to_all(
        q_local.astype(jnp.bfloat16), "head", split_axis=1, concat_axis=0, tiled=True
    ).astype(q_local.dtype)
    own_table = slot_table(policy[:, 0], seq_dev, CAPP, POLICIES).astype(jnp.float32)
    q_values = jnp.dot(
        own_table.T,
        returned.reshape(POLICIES * CAPP, learn * ACTIONS),
        precision=lax.Precision.HIGHEST,
    ).reshape(seq_dev, learn, ACTIONS)
    chosen = actions[:, :, None] == jnp.arange(ACTIONS, dtype=jnp.int32)[None, None, :]
    q_taken = jnp.sum(jnp.where(chosen, q_values, 0.0), axis=-1)
    return (q_values, q_taken)


def solution(mesh):
    return jax.shard_map(
        shards,
        mesh=mesh,
        in_specs=(
            P(("batch", "head"), None, None),
            P(("batch", "head"), None),
            P(("batch", "head"), None),
            P(("batch", "head")),
            P(("batch", "head"), None),
            P(("batch", "head"), None),
            P(("batch", "head"), None),
            P("batch", None, "head"),
            P("batch", None, "head"),
            P(),
            P("head", None, None),
            P("head", None),
            P("head", None, None),
        ),
        out_specs=(P(("batch", "head"), None, None), P(("batch", "head"), None)),
        check_vma=False,
    )
```

profile of v0, /device:TPU:0, one launch (start us, length us, event | category | flops | bytes accessed | tf_op | source)
XLA Modules:
  0.0 445.9 jit_solution(649766315634340554)
XLA Ops:
  10.8 6.3 %all-gather = bf16[4,32,24]{1,2,0:T(8,128)(2,1)S(1)} all-gather(bf16[1,32,24]{1,2,0:T(8,128)(2,1)S(1)} %convert_bitcast_fusion.1), channel_id=1, replica_groups=mesh['batch'=8,'head'=4] {'head'}, dimensions={0}, use_global_device_ids=true | all-gather | bytes 7680 | tf_op jit(solution)/shard_map/all_gather | solution.py:73
  19.9 7.9 %all-reduce = bf16[128]{0:T(256)(128)(2,1)S(1)} all-reduce(bf16[128]{0:T(256)(128)(2,1)S(1)} %dynamic-update-slice), channel_id=1, replica_groups=mesh['batch'=8,'head'=4] {'head'}, use_global_device_ids=true, to_apply=%add | all-reduce | flops 128 | bytes 512
  41.3 11.8 %all-gather.7.cloned.1.call-done = bf16[512,4,256]{2,1,0:T(4,128)(2,1)} async-done(((bf16[64,4,256]{2,1,0:T(4,128)(2,1)}), bf16[512,4,256]{2,1,0:T(4,128)(2,1)}) %all-gather.7.cloned.1.call-update) | async-done | bytes 1048592 | tf_op jit(solution)/shard_map/all_gather | solution.py:68
  54.8 48.3 %all-gather.9.cloned.1.call-done = bf16[1024,4,256]{2,1,0:T(4,128)(2,1)} async-done(((bf16[128,4,256]{2,1,0:T(4,128)(2,1)}), bf16[1024,4,256]{2,1,0:T(4,128)(2,1)}) %all-gather.9.cloned.1.call-update) | async-done | bytes 2097168 | tf_op jit(solution)/shard_map/all_gather | solution.py:69
  105.2 26.6 %all-gather.5.cloned.1.call-done = bf16[128,24,512]{2,1,0:T(8,128)(2,1)} async-done(((bf16[32,24,512]{2,1,0:T(8,128)(2,1)}), bf16[128,24,512]{2,1,0:T(8,128)(2,1)}) %all-gather.5.cloned.1.call-update) | async-done | bytes 3145744 | tf_op jit(solution)/shard_map/all_gather | solution.py:72
  131.7 8.4 %fusion.22 = f32[24,128,4,256]{3,0,2,1:T(8,128)} fusion(bf16[128,24,512]{2,1,0:T(8,128)(2,1)} %all-gather.5.cloned.1.call-done, bf16[512,4,256]{0,2,1:T(8,128)(2,1)S(1)} %copy.72), kind=kOutput, calls=%fused_computation.32 | convolution fusion | flops 3221225472 | bytes 16777216 | tf_op jit(solution)/shard_map/dot_general | solution.py:79
  140.1 239.5 %while.14 = (s32[]{:T(128)}, bf16[128,256]{1,0:T(8,128)(2,1)S(1)}, f32[128,256]{1,0:T(8,128)S(1)}, bf16[24,128,256]{2,1,0:T(8,128)(2,1)}, f32[24,128,4,256]{3,0,...) while((s32[]{:T(128)}, bf16[128,256]{1,0:T(8,128)(2,1)S(1)}, ...), condition=%wide.region_3.4_spmd, body=%wide.region_2.3_spmd.sunk | while | flops 269320320 | bytes 6756965 | solution.py:97
  150.0 5.8 %all_gather.32 = bf16[128,1024]{1,0:T(8,128)(2,1)S(1)} all-gather(bf16[128,256]{1,0:T(8,128)(2,1)S(1)} %get-tuple-element.175), channel_id=1, replica_groups=mesh['batch'=8,'head'=4] {'head'}, dimensions={1}, use_global_device_ids=true | all-gather | bytes 327680 | tf_op jit(solution)/shard_map/while/body/eval_jaxpr/all_gather | solution.py:93
  190.0 5.8 %all_gather.32 = bf16[128,1024]{1,0:T(8,128)(2,1)S(1)} all-gather(bf16[128,256]{1,0:T(8,128)(2,1)S(1)} %get-tuple-element.175), channel_id=1, replica_groups=mesh['batch'=8,'head'=4] {'head'}, dimensions={1}, use_global_device_ids=true | all-gather | bytes 327680 | tf_op jit(solution)/shard_map/while/body/eval_jaxpr/all_gather | solution.py:93
  199.9 5.8 %all_gather.32 = bf16[128,1024]{1,0:T(8,128)(2,1)S(1)} all-gather(bf16[128,256]{1,0:T(8,128)(2,1)S(1)} %get-tuple-element.175), channel_id=1, replica_groups=mesh['batch'=8,'head'=4] {'head'}, dimensions={1}, use_global_device_ids=true | all-gather | bytes 327680 | tf_op jit(solution)/shard_map/while/body/eval_jaxpr/all_gather | solution.py:93
  209.9 5.8 %all_gather.32 = bf16[128,1024]{1,0:T(8,128)(2,1)S(1)} all-gather(bf16[128,256]{1,0:T(8,128)(2,1)S(1)} %get-tuple-element.175), channel_id=1, replica_groups=mesh['batch'=8,'head'=4] {'head'}, dimensions={1}, use_global_device_ids=true | all-gather | bytes 327680 | tf_op jit(solution)/shard_map/while/body/eval_jaxpr/all_gather | solution.py:93
  219.9 5.8 %all_gather.32 = bf16[128,1024]{1,0:T(8,128)(2,1)S(1)} all-gather(bf16[128,256]{1,0:T(8,128)(2,1)S(1)} %get-tuple-element.175), channel_id=1, replica_groups=mesh['batch'=8,'head'=4] {'head'}, dimensions={1}, use_global_device_ids=true | all-gather | bytes 327680 | tf_op jit(solution)/shard_map/while/body/eval_jaxpr/all_gather | solution.py:93
  229.9 5.8 %all_gather.32 = bf16[128,1024]{1,0:T(8,128)(2,1)S(1)} all-gather(bf16[128,256]{1,0:T(8,128)(2,1)S(1)} %get-tuple-element.175), channel_id=1, replica_groups=mesh['batch'=8,'head'=4] {'head'}, dimensions={1}, use_global_device_ids=true | all-gather | bytes 327680 | tf_op jit(solution)/shard_map/while/body/eval_jaxpr/all_gather | solution.py:93
  249.9 5.8 %all_gather.32 = bf16[128,1024]{1,0:T(8,128)(2,1)S(1)} all-gather(bf16[128,256]{1,0:T(8,128)(2,1)S(1)} %get-tuple-element.175), channel_id=1, replica_groups=mesh['batch'=8,'head'=4] {'head'}, dimensions={1}, use_global_device_ids=true | all-gather | bytes 327680 | tf_op jit(solution)/shard_map/while/body/eval_jaxpr/all_gather | solution.py:93
  259.9 5.8 %all_gather.32 = bf16[128,1024]{1,0:T(8,128)(2,1)S(1)} all-gather(bf16[128,256]{1,0:T(8,128)(2,1)S(1)} %get-tuple-element.175), channel_id=1, replica_groups=mesh['batch'=8,'head'=4] {'head'}, dimensions={1}, use_global_device_ids=true | all-gather | bytes 327680 | tf_op jit(solution)/shard_map/while/body/eval_jaxpr/all_gather | solution.py:93
  269.9 5.8 %all_gather.32 = bf16[128,1024]{1,0:T(8,128)(2,1)S(1)} all-gather(bf16[128,256]{1,0:T(8,128)(2,1)S(1)} %get-tuple-element.175), channel_id=1, replica_groups=mesh['batch'=8,'head'=4] {'head'}, dimensions={1}, use_global_device_ids=true | all-gather | bytes 327680 | tf_op jit(solution)/shard_map/while/body/eval_jaxpr/all_gather | solution.py:93
  289.8 5.8 %all_gather.32 = bf16[128,1024]{1,0:T(8,128)(2,1)S(1)} all-gather(bf16[128,256]{1,0:T(8,128)(2,1)S(1)} %get-tuple-element.175), channel_id=1, replica_groups=mesh['batch'=8,'head'=4] {'head'}, dimensions={1}, use_global_device_ids=true | all-gather | bytes 327680 | tf_op jit(solution)/shard_map/while/body/eval_jaxpr/all_gather | solution.py:93
  299.8 5.8 %all_gather.32 = bf16[128,1024]{1,0:T(8,128)(2,1)S(1)} all-gather(bf16[128,256]{1,0:T(8,128)(2,1)S(1)} %get-tuple-element.175), channel_id=1, replica_groups=mesh['batch'=8,'head'=4] {'head'}, dimensions={1}, use_global_device_ids=true | all-gather | bytes 327680 | tf_op jit(solution)/shard_map/while/body/eval_jaxpr/all_gather | solution.py:93
  309.8 5.8 %all_gather.32 = bf16[128,1024]{1,0:T(8,128)(2,1)S(1)} all-gather(bf16[128,256]{1,0:T(8,128)(2,1)S(1)} %get-tuple-element.175), channel_id=1, replica_groups=mesh['batch'=8,'head'=4] {'head'}, dimensions={1}, use_global_device_ids=true | all-gather | bytes 327680 | tf_op jit(solution)/shard_map/while/body/eval_jaxpr/all_gather | solution.py:93
  319.8 5.8 %all_gather.32 = bf16[128,1024]{1,0:T(8,128)(2,1)S(1)} all-gather(bf16[128,256]{1,0:T(8,128)(2,1)S(1)} %get-tuple-element.175), channel_id=1, replica_groups=mesh['batch'=8,'head'=4] {'head'}, dimensions={1}, use_global_device_ids=true | all-gather | bytes 327680 | tf_op jit(solution)/shard_map/while/body/eval_jaxpr/all_gather | solution.py:93
  329.8 5.8 %all_gather.32 = bf16[128,1024]{1,0:T(8,128)(2,1)S(1)} all-gather(bf16[128,256]{1,0:T(8,128)(2,1)S(1)} %get-tuple-element.175), channel_id=1, replica_groups=mesh['batch'=8,'head'=4] {'head'}, dimensions={1}, use_global_device_ids=true | all-gather | bytes 327680 | tf_op jit(solution)/shard_map/while/body/eval_jaxpr/all_gather | solution.py:93
  339.7 5.8 %all_gather.32 = bf16[128,1024]{1,0:T(8,128)(2,1)S(1)} all-gather(bf16[128,256]{1,0:T(8,128)(2,1)S(1)} %get-tuple-element.175), channel_id=1, replica_groups=mesh['batch'=8,'head'=4] {'head'}, dimensions={1}, use_global_device_ids=true | all-gather | bytes 327680 | tf_op jit(solution)/shard_map/while/body/eval_jaxpr/all_gather | solution.py:93
  387.3 25.3 %all-to-all-done = bf16[32,8,16,256]{3,1,2,0:T(8,128)(2,1)S(1)} async-done(((bf16[32,8,16,256]{3,1,2,0:T(8,128)(2,1)}), bf16[32,8,16,256]{3,1,2,0:T(8,128)(2,1)S(1)}, u32[]{:S(2)}, u32[]{:S(2)}) %all-to-all-start) | async-done | bytes 2097184 | tf_op jit(solution)/shard_map/all_to_all | solution.py:104
  418.8 8.2 %maximum_convert_fusion = bf16[8,128,1024]{2,1,0:T(8,128)(2,1)S(1)} fusion(bf16[8,128,1024]{2,1,0:T(8,128)(2,1)S(1)} %reshape.154, bf16[8,1024,1024]{2,1,0:T(8,128)(2,1)} %param.25), kind=kOutput, calls=%fused_computation.31 | convolution fusion | flops 2149580800 | bytes 20971520 | tf_op jit(solution)/shard_map/prh,phk->prk/dot_general | solution.py:107
  (189 shorter events, 200.5 us)
Async XLA Ops:
  7.2 419.8 %copy-start = (bf16[8,512,18]{1,0,2:T(8,128)(2,1)S(1)}, bf16[8,512,18]{1,0,2:T(8,128)(2,1)}, u32[]{:S(2)}) copy-start(bf16[8,512,18]{1,0,2:T(8,128)(2,1)} %param.27) | copy-start | bytes 442372
  7.2 46.0 %all-gather.7.cloned.1.call-start = ((), (), s32[]{:S(2)}) async-start(), calls=%async_computation.3 | async-start | bytes 1179648 | tf_op jit(solution)/shard_map/all_gather | solution.py:68
  7.9 95.2 %all-gather.9.cloned.1.call-start = ((), (), s32[]{:S(2)}) async-start(), calls=%async_computation.4 | async-start | bytes 2359296 | tf_op jit(solution)/shard_map/all_gather | solution.py:69
  8.7 123.1 %all-gather.5.cloned.1.call-start = ((), (), s32[]{:S(2)}) async-start(), calls=%async_computation.2 | async-start | bytes 3932160 | tf_op jit(solution)/shard_map/all_gather | solution.py:72
  383.2 3.9 copy-start.2
  383.2 29.4 %all-to-all-start = ((bf16[32,8,16,256]{3,1,2,0:T(8,128)(2,1)}), bf16[32,8,16,256]{3,1,2,0:T(8,128)(2,1)S(1)}, u32[]{:S(2)}, u32[]{:S(2)}) async-start(bf16[32,8,16,256]{3,1,2,0:T(8,128)(2,1)} %copy.61), calls=%async_computation | async-start | bytes 4194304 | tf_op jit(solution)/shard_map/all_to_all | solution.py:104
  418.8 8.6 %copy-start.3 = (bf16[8,512]{1,0:T(8,128)(2,1)S(1)}, bf16[8,512]{1,0:T(8,128)(2,1)}, u32[]{:S(2)}) copy-start(bf16[8,512]{1,0:T(8,128)(2,1)} %param.26) | copy-start | bytes 24580
  427.4 10.4 %copy-start.1 = (s32[32,16]{0,1:T(8,128)S(1)}, s32[32,16]{0,1:T(8,128)}, u32[]{:S(2)}) copy-start(s32[32,16]{0,1:T(8,128)} %param.21) | copy-start | bytes 6148
  429.6 7.2 %all-to-all-start.1 = ((bf16[4,2,2304]{2,1,0:T(2,128)(2,1)}), bf16[4,2,2304]{2,1,0:T(2,128)(2,1)S(1)}, u32[]{:S(2)}, u32[]{:S(2)}) async-start(bf16[4,2,2304]{2,1,0:T(2,128)(2,1)} %reshape.177), calls=%async_computation.1 | async-start | bytes 73728 | tf_op jit(solution)/shard_map/all_to_all | solution.py:118
Sparse Core Ops, SparseCore 0:
  10.1 42.9 all-gather.6
  55.3 47.7 all-gather.8
  104.7 27.0 all-gather.4
where the time goes:
time: 448 us; the launch traced here: 446 us
  blocking collectives  166 us (37%)
  waiting for transfers between devices  118 us (26%)
  local copies, waits for them, and re-layouts  82.5 us (18%)
  matrix products  31.8 us (7%)
  other arithmetic  25.4 us (6%)
  between operations  14.6 us (3%)
  starting transfers between devices  7.3 us (2%)
    all_gather x24, blocking collectives, advance(): full_h = lax.all_gather(part_h, 'head', axis=1, tiled=True)  140 us
    dynamic_slice x24, local copies, waits for them, and re-layouts, shards(): _, outputs = lax.scan(advance, (part_h, part_c), (pre, keeps))  65.2 us
    all_gather x1, waiting for transfers between devices, shards(): lax.all_gather(w_recur, 'batch', axis=0, tiled=True)  48.3 us
    all_gather x1, waiting for transfers between devices, shards(): lax.all_gather(features, 'head', axis=0, tiled=True)  26.6 us
    all_to_all x1, waiting for transfers between devices, shards(): lax.all_to_all(packed, 'head', split_axis=0, concat_axis=3, tiled=True)  25.3 us
    dynamic_update_slice x24, other arithmetic, shards(): _, outputs = lax.scan(advance, (part_h, part_c), (pre, keeps))  19.1 us
    all_gather x1, waiting for transfers between devices, shards(): lax.all_gather(w_input, 'batch', axis=0, tiled=True)  11.8 us
    dot_general x24, matrix products, lstm_cell(): jnp.dot(full_h, w_flat, preferred_element_type=jnp.float32)  11.7 us
  transfers between devices with their start and end apart: 5, of which 5 were waited for; matrix products, arithmetic and copies ran while one was open for 2% of the time, Pallas kernels for 0%

commit v1 on v0

--- a/solution.py
+++ b/solution.py
@@ -90,7 +90,7 @@
     def advance(carry, inputs):
         part_h, part_c = carry
         pre_t, keep_t = inputs
-        full_h = lax.all_gather(part_h, "head", axis=1, tiled=True)
+        full_h = jnp.concatenate(lax.all_gather(part_h, "head"), axis=1)
         new_h, part_c = lstm_cell(pre_t, full_h, part_c, keep_t, w_flat, bias, quarter)
         return ((new_h, part_c), new_h)
 

time: 448 us -> 425 us (0.949)
  local copies, waits for them, and re-layouts: 82.5 us -> 27.2 us
  matrix products: 31.8 us -> 65.5 us
    dynamic_slice x24 -> x0, local copies, waits for them, and re-layouts: 65.2 us -> none  [shards(): _, outputs = lax.scan(advance, (part_h, part_c), (pre, keeps))]
    dot_general x24, matrix products: 11.7 us -> 45.1 us  [lstm_cell(): jnp.dot(full_h, w_flat, preferred_element_type=jnp.float32)]
    mul x0 -> x48, local copies, waits for them, and re-layouts: none -> 9.06 us  [lstm_cell(): full_h = full_h * keep_t[:, None].astype(jnp.bfloat16)]
where the time goes in v1:
time: 425 us; the launch traced here: 423 us
  blocking collectives  166 us (39%)
  waiting for transfers between devices  117 us (28%)
  matrix products  65.5 us (15%)
  local copies, waits for them, and re-layouts  27.2 us (6%)
  other arithmetic  24.8 us (6%)
  between operations  14.6 us (3%)
  starting transfers between devices  7.3 us (2%)
    all_gather x24, blocking collectives, advance(): full_h = jnp.concatenate(lax.all_gather(part_h, 'head'), axis=1)  140 us
    all_gather x1, waiting for transfers between devices, shards(): lax.all_gather(w_recur, 'batch', axis=0, tiled=True)  48.3 us
    dot_general x24, matrix products, lstm_cell(): jnp.dot(full_h, w_flat, preferred_element_type=jnp.float32)  45.1 us
    all_gather x1, waiting for transfers between devices, shards(): lax.all_gather(features, 'head', axis=0, tiled=True)  25.7 us
    all_to_all x1, waiting for transfers between devices, shards(): lax.all_to_all(packed, 'head', split_axis=0, concat_axis=3, tiled=True)  25.3 us
    dynamic_update_slice x24, other arithmetic, shards(): _, outputs = lax.scan(advance, (part_h, part_c), (pre, keeps))  19.2 us
    all_gather x1, waiting for transfers between devices, shards(): lax.all_gather(w_input, 'batch', axis=0, tiled=True)  11.8 us
    mul x48, local copies, waits for them, and re-layouts, lstm_cell(): full_h = full_h * keep_t[:, None].astype(jnp.bfloat16)  9.06 us
  transfers between devices with their start and end apart: 5, of which 5 were waited for; matrix products, arithmetic and copies ran while one was open for 2% of the time, Pallas kernels for 0%

profile of v1, /device:TPU:0, one launch (start us, length us, event | category | flops | bytes accessed | tf_op | source)
XLA Modules:
  0.0 422.9 jit_solution(15213633172910885321)
XLA Ops:
  10.8 6.3 %all-gather.1 = bf16[4,32,24]{1,2,0:T(8,128)(2,1)S(1)} all-gather(bf16[1,32,24]{1,2,0:T(8,128)(2,1)S(1)} %convert_bitcast_fusion.1), channel_id=1, replica_groups=mesh['batch'=8,'head'=4] {'head'}, dimensions={0}, use_global_device_ids=true | all-gather | bytes 7680 | tf_op jit(solution)/shard_map/all_gather | solution.py:73
  19.9 7.9 %all-reduce = bf16[128]{0:T(256)(128)(2,1)S(1)} all-reduce(bf16[128]{0:T(256)(128)(2,1)S(1)} %dynamic-update-slice), channel_id=1, replica_groups=mesh['batch'=8,'head'=4] {'head'}, use_global_device_ids=true, to_apply=%add | all-reduce | flops 128 | bytes 512
  41.3 11.8 %all-gather.10.cloned.1.call-done = bf16[512,4,256]{2,1,0:T(4,128)(2,1)} async-done(((bf16[64,4,256]{2,1,0:T(4,128)(2,1)}), bf16[512,4,256]{2,1,0:T(4,128)(2,1)}) %all-gather.10.cloned.1.call-update) | async-done | bytes 1048592 | tf_op jit(solution)/shard_map/all_gather | solution.py:68
  54.8 48.3 %all-gather.12.cloned.1.call-done = bf16[1024,4,256]{2,1,0:T(4,128)(2,1)} async-done(((bf16[128,4,256]{2,1,0:T(4,128)(2,1)}), bf16[1024,4,256]{2,1,0:T(4,128)(2,1)}) %all-gather.12.cloned.1.call-update) | async-done | bytes 2097168 | tf_op jit(solution)/shard_map/all_gather | solution.py:69
  106.1 25.7 %all-gather.8.cloned.1.call-done = bf16[128,24,512]{2,1,0:T(8,128)(2,1)} async-done(((bf16[32,24,512]{2,1,0:T(8,128)(2,1)}), bf16[128,24,512]{2,1,0:T(8,128)(2,1)}) %all-gather.8.cloned.1.call-update) | async-done | bytes 3145744 | tf_op jit(solution)/shard_map/all_gather | solution.py:72
  131.7 8.7 %fusion.19 = f32[24,128,4,256]{3,1,2,0:T(8,128)} fusion(bf16[128,24,512]{2,1,0:T(8,128)(2,1)} %all-gather.8.cloned.1.call-done, bf16[512,4,256]{0,2,1:T(8,128)(2,1)S(1)} %copy.72), kind=kOutput, calls=%fused_computation.28 | convolution fusion | flops 3221225472 | bytes 16777216 | tf_op jit(solution)/shard_map/dot_general | solution.py:79
  140.5 216.2 %while.14 = (s32[]{:T(128)}, bf16[128,256]{1,0:T(8,128)(2,1)S(1)}, f32[128,256]{1,0:T(8,128)S(1)}, bf16[24,128,256]{2,1,0:T(8,128)(2,1)}, f32[24,128,4,256]{3,1,...) while((s32[]{:T(128)}, bf16[128,256]{1,0:T(8,128)(2,1)S(1)}, ...), condition=%wide.region_3.4_spmd, body=%wide.region_2.3_spmd.sunk | while | flops 269320320 | bytes 6232677 | solution.py:97
  149.4 5.8 %all-gather.3 = bf16[512,256]{1,0:T(8,128)(2,1)S(1)} all-gather(bf16[128,256]{1,0:T(8,128)(2,1)S(1)} %get-tuple-element.175), channel_id=2, replica_groups=mesh['batch'=8,'head'=4] {'head'}, dimensions={0}, use_global_device_ids=true | all-gather | bytes 327680 | tf_op jit(solution)/shard_map/while/body/eval_jaxpr/all_gather | solution.py:93
  158.4 5.8 %all-gather.3 = bf16[512,256]{1,0:T(8,128)(2,1)S(1)} all-gather(bf16[128,256]{1,0:T(8,128)(2,1)S(1)} %get-tuple-element.175), channel_id=2, replica_groups=mesh['batch'=8,'head'=4] {'head'}, dimensions={0}, use_global_device_ids=true | all-gather | bytes 327680 | tf_op jit(solution)/shard_map/while/body/eval_jaxpr/all_gather | solution.py:93
  167.4 5.8 %all-gather.3 = bf16[512,256]{1,0:T(8,128)(2,1)S(1)} all-gather(bf16[128,256]{1,0:T(8,128)(2,1)S(1)} %get-tuple-element.175), channel_id=2, replica_groups=mesh['batch'=8,'head'=4] {'head'}, dimensions={0}, use_global_device_ids=true | all-gather | bytes 327680 | tf_op jit(solution)/shard_map/while/body/eval_jaxpr/all_gather | solution.py:93
  176.4 5.8 %all-gather.3 = bf16[512,256]{1,0:T(8,128)(2,1)S(1)} all-gather(bf16[128,256]{1,0:T(8,128)(2,1)S(1)} %get-tuple-element.175), channel_id=2, replica_groups=mesh['batch'=8,'head'=4] {'head'}, dimensions={0}, use_global_device_ids=true | all-gather | bytes 327680 | tf_op jit(solution)/shard_map/while/body/eval_jaxpr/all_gather | solution.py:93
  185.4 5.8 %all-gather.3 = bf16[512,256]{1,0:T(8,128)(2,1)S(1)} all-gather(bf16[128,256]{1,0:T(8,128)(2,1)S(1)} %get-tuple-element.175), channel_id=2, replica_groups=mesh['batch'=8,'head'=4] {'head'}, dimensions={0}, use_global_device_ids=true | all-gather | bytes 327680 | tf_op jit(solution)/shard_map/while/body/eval_jaxpr/all_gather | solution.py:93
  203.4 5.8 %all-gather.3 = bf16[512,256]{1,0:T(8,128)(2,1)S(1)} all-gather(bf16[128,256]{1,0:T(8,128)(2,1)S(1)} %get-tuple-element.175), channel_id=2, replica_groups=mesh['batch'=8,'head'=4] {'head'}, dimensions={0}, use_global_device_ids=true | all-gather | bytes 327680 | tf_op jit(solution)/shard_map/while/body/eval_jaxpr/all_gather | solution.py:93
  212.4 5.8 %all-gather.3 = bf16[512,256]{1,0:T(8,128)(2,1)S(1)} all-gather(bf16[128,256]{1,0:T(8,128)(2,1)S(1)} %get-tuple-element.175), channel_id=2, replica_groups=mesh['batch'=8,'head'=4] {'head'}, dimensions={0}, use_global_device_ids=true | all-gather | bytes 327680 | tf_op jit(solution)/shard_map/while/body/eval_jaxpr/all_gather | solution.py:93
  230.5 5.8 %all-gather.3 = bf16[512,256]{1,0:T(8,128)(2,1)S(1)} all-gather(bf16[128,256]{1,0:T(8,128)(2,1)S(1)} %get-tuple-element.175), channel_id=2, replica_groups=mesh['batch'=8,'head'=4] {'head'}, dimensions={0}, use_global_device_ids=true | all-gather | bytes 327680 | tf_op jit(solution)/shard_map/while/body/eval_jaxpr/all_gather | solution.py:93
  239.5 5.8 %all-gather.3 = bf16[512,256]{1,0:T(8,128)(2,1)S(1)} all-gather(bf16[128,256]{1,0:T(8,128)(2,1)S(1)} %get-tuple-element.175), channel_id=2, replica_groups=mesh['batch'=8,'head'=4] {'head'}, dimensions={0}, use_global_device_ids=true | all-gather | bytes 327680 | tf_op jit(solution)/shard_map/while/body/eval_jaxpr/all_gather | solution.py:93
  248.5 5.8 %all-gather.3 = bf16[512,256]{1,0:T(8,128)(2,1)S(1)} all-gather(bf16[128,256]{1,0:T(8,128)(2,1)S(1)} %get-tuple-element.175), channel_id=2, replica_groups=mesh['batch'=8,'head'=4] {'head'}, dimensions={0}, use_global_device_ids=true | all-gather | bytes 327680 | tf_op jit(solution)/shard_map/while/body/eval_jaxpr/all_gather | solution.py:93
  266.6 5.8 %all-gather.3 = bf16[512,256]{1,0:T(8,128)(2,1)S(1)} all-gather(bf16[128,256]{1,0:T(8,128)(2,1)S(1)} %get-tuple-element.175), channel_id=2, replica_groups=mesh['batch'=8,'head'=4] {'head'}, dimensions={0}, use_global_device_ids=true | all-gather | bytes 327680 | tf_op jit(solution)/shard_map/while/body/eval_jaxpr/all_gather | solution.py:93
  275.6 5.8 %all-gather.3 = bf16[512,256]{1,0:T(8,128)(2,1)S(1)} all-gather(bf16[128,256]{1,0:T(8,128)(2,1)S(1)} %get-tuple-element.175), channel_id=2, replica_groups=mesh['batch'=8,'head'=4] {'head'}, dimensions={0}, use_global_device_ids=true | all-gather | bytes 327680 | tf_op jit(solution)/shard_map/while/body/eval_jaxpr/all_gather | solution.py:93
  311.6 5.8 %all-gather.3 = bf16[512,256]{1,0:T(8,128)(2,1)S(1)} all-gather(bf16[128,256]{1,0:T(8,128)(2,1)S(1)} %get-tuple-element.175), channel_id=2, replica_groups=mesh['batch'=8,'head'=4] {'head'}, dimensions={0}, use_global_device_ids=true | all-gather | bytes 327680 | tf_op jit(solution)/shard_map/while/body/eval_jaxpr/all_gather | solution.py:93
  320.6 5.8 %all-gather.3 = bf16[512,256]{1,0:T(8,128)(2,1)S(1)} all-gather(bf16[128,256]{1,0:T(8,128)(2,1)S(1)} %get-tuple-element.175), channel_id=2, replica_groups=mesh['batch'=8,'head'=4] {'head'}, dimensions={0}, use_global_device_ids=true | all-gather | bytes 327680 | tf_op jit(solution)/shard_map/while/body/eval_jaxpr/all_gather | solution.py:93
  338.6 5.8 %all-gather.3 = bf16[512,256]{1,0:T(8,128)(2,1)S(1)} all-gather(bf16[128,256]{1,0:T(8,128)(2,1)S(1)} %get-tuple-element.175), channel_id=2, replica_groups=mesh['batch'=8,'head'=4] {'head'}, dimensions={0}, use_global_device_ids=true | all-gather | bytes 327680 | tf_op jit(solution)/shard_map/while/body/eval_jaxpr/all_gather | solution.py:93
  364.3 25.3 %all-to-all-done = bf16[32,8,16,256]{3,1,2,0:T(8,128)(2,1)S(1)} async-done(((bf16[32,8,16,256]{3,1,2,0:T(8,128)(2,1)}), bf16[32,8,16,256]{3,1,2,0:T(8,128)(2,1)S(1)}, u32[]{:S(2)}, u32[]{:S(2)}) %all-to-all-start) | async-done | bytes 2097184 | tf_op jit(solution)/shard_map/all_to_all | solution.py:104
  395.8 8.2 %maximum_convert_fusion = bf16[8,128,1024]{2,1,0:T(8,128)(2,1)S(1)} fusion(bf16[8,128,1024]{2,1,0:T(8,128)(2,1)S(1)} %reshape.161, bf16[8,1024,1024]{2,1,0:T(8,128)(2,1)} %param.25), kind=kOutput, calls=%fused_computation.27 | convolution fusion | flops 2149580800 | bytes 20971520 | tf_op jit(solution)/shard_map/prh,phk->prk/dot_general | solution.py:107
  (213 shorter events, 177.9 us)
Async XLA Ops:
  7.2 396.8 %copy-start = (bf16[8,512,18]{1,0,2:T(8,128)(2,1)S(1)}, bf16[8,512,18]{1,0,2:T(8,128)(2,1)}, u32[]{:S(2)}) copy-start(bf16[8,512,18]{1,0,2:T(8,128)(2,1)} %param.27) | copy-start | bytes 442372
  7.2 46.0 %all-gather.10.cloned.1.call-start = ((), (), s32[]{:S(2)}) async-start(), calls=%async_computation.3 | async-start | bytes 1179648 | tf_op jit(solution)/shard_map/all_gather | solution.py:68
  7.9 95.2 %all-gather.12.cloned.1.call-start = ((), (), s32[]{:S(2)}) async-start(), calls=%async_computation.4 | async-start | bytes 2359296 | tf_op jit(solution)/shard_map/all_gather | solution.py:69
  8.7 123.1 %all-gather.8.cloned.1.call-start = ((), (), s32[]{:S(2)}) async-start(), calls=%async_computation.2 | async-start | bytes 3932160 | tf_op jit(solution)/shard_map/all_gather | solution.py:72
  360.1 3.9 copy-start.2
  360.1 29.4 %all-to-all-start = ((bf16[32,8,16,256]{3,1,2,0:T(8,128)(2,1)}), bf16[32,8,16,256]{3,1,2,0:T(8,128)(2,1)S(1)}, u32[]{:S(2)}, u32[]{:S(2)}) async-start(bf16[32,8,16,256]{3,1,2,0:T(8,128)(2,1)} %copy.61), calls=%async_computation | async-start | bytes 4194304 | tf_op jit(solution)/shard_map/all_to_all | solution.py:104
  395.8 8.6 %copy-start.3 = (bf16[8,512]{1,0:T(8,128)(2,1)S(1)}, bf16[8,512]{1,0:T(8,128)(2,1)}, u32[]{:S(2)}) copy-start(bf16[8,512]{1,0:T(8,128)(2,1)} %param.26) | copy-start | bytes 24580
  404.4 10.4 %copy-start.1 = (s32[32,16]{0,1:T(8,128)S(1)}, s32[32,16]{0,1:T(8,128)}, u32[]{:S(2)}) copy-start(s32[32,16]{0,1:T(8,128)} %param.21) | copy-start | bytes 6148
  406.6 7.2 %all-to-all-start.1 = ((bf16[4,2,2304]{2,1,0:T(2,128)(2,1)}), bf16[4,2,2304]{2,1,0:T(2,128)(2,1)S(1)}, u32[]{:S(2)}, u32[]{:S(2)}) async-start(bf16[4,2,2304]{2,1,0:T(2,128)(2,1)} %reshape.187), calls=%async_computation.1 | async-start | bytes 73728 | tf_op jit(solution)/shard_map/all_to_all | solution.py:118
Sparse Core Ops, SparseCore 0:
  10.1 42.9 all-gather.9
  55.3 47.7 all-gather.11
  104.7 27.0 all-gather.7
